TPU v7x, 32 devices: a whole 2x2x4 slice. The times are simulated.
32 devices in a mesh: dp: 4 (over y, x), expert: 4 (over z), tensor: 2 (over core).
Axes of the slice: x: 2, y: 2, z: 4, core: 2. Of those that a mesh axis runs over, the one named last changes fastest.
Arguments:
- tokens: bfloat16 [2048, 2560], P(('dp', 'expert')), may hold values from -6 to 6
- norm_gain: float32 [2560], replicated, may hold values from 0.5 to 1.5
- expert_ids: int32 [2048, 6], P(('dp', 'expert')), may hold values from 0 to 31, all different within a row; in each aligned block of 128 rows (0 to 127, 128 to 255, ...) at most 48 rows name the same one
- route_weights: int32 [2048, 6], P(('dp', 'expert')), may hold values from 1 to 64
- w_gate: bfloat16 [32, 2560, 768], P('expert', None, 'tensor'), may hold values from -0.125 to 0.125
- w_up: bfloat16 [32, 2560, 768], P('expert', None, 'tensor'), may hold values from -0.125 to 0.125
- w_down: bfloat16 [32, 768, 2560], P('expert', 'tensor'), may hold values from -0.21875 to 0.21875
- shared_gate: bfloat16 [2560, 2048], P(None, ('dp', 'tensor')), may hold values from -0.125 to 0.125
- shared_up: bfloat16 [2560, 2048], P(None, ('dp', 'tensor')), may hold values from -0.125 to 0.125
- shared_down: bfloat16 [2048, 2560], P(('dp', 'tensor')), may hold values from -0.125 to 0.125
Outputs:
- mixed: bfloat16 [2048, 2560], P(('dp', 'expert'), 'tensor')
Inputs may be any that keep to these rules, and one draw needn't show every extreme that they name: `expert_ids`: each row names 6 different experts. In each aligned block of 128 rows (the rows of one index of dp+expert) no expert is named by more than 48 rows, a bound that some blocks reach.
All inputs are finite; a program needn't handle non-finite values.
Results may differ from a plain program's by a relative error of at most 0.011.
Values may be sent and summed in bfloat16 or wider, within the bound.
A program may use at most 128 MiB of HBM per device.

v0:
```python
import jax
import jax.numpy as jnp
from jax import lax
from jax.sharding import PartitionSpec as P

EPSILON = 1e-06
LANES = 128


def normalize(tokens, norm_gain):
    values = tokens.astype(jnp.float32)
    inverse = lax.rsqrt(jnp.mean(values * values, axis=1, keepdims=True) + EPSILON)
    return (values * inverse * norm_gain[None, :]).astype(jnp.bfloat16)


def by_owner(partial, blocks, width):
    rows = partial.shape[0] // blocks
    parts = partial.shape[1] // width
    split = partial.reshape(blocks, rows, parts, width)
    return split.transpose(0, 2, 1, 3).reshape(blocks * parts * rows, width)


def on_device(
    tokens,
    norm_gain,
    expert_ids,
    route_weights,
    w_gate,
    w_up,
    w_down,
    shared_gate,
    shared_up,
    shared_down,
):
    normed = normalize(tokens, norm_gain)
    rows, width = normed.shape
    owners = lax.axis_size("expert")
    groups = lax.axis_size("dp")
    half = width // lax.axis_size("tensor")
    local = w_gate.shape[0]
    experts = local * owners
    lanes = -(-experts // LANES) * LANES
    match = expert_ids[:, :, None] == jnp.arange(lanes, dtype=jnp.int32)[None, None, :]
    scale = jnp.sum(jnp.where(match, route_weights[:, :, None], 0), axis=1)
    scale = (scale.astype(jnp.float32) / 64.0).astype(jnp.bfloat16)
    sent = jnp.concatenate([normed, scale], axis=1)
    everyone = lax.all_gather(sent, "expert", axis=0, tiled=True)
    routed_rows = everyone[:, :width]
    first = lax.axis_index("expert") * local
    mine = lax.dynamic_slice_in_dim(everyone[:, width:], first, local, 1).astype(jnp.float32)
    hidden = []
    for e in range(local):
        gate = jnp.dot(routed_rows, w_gate[e], preferred_element_type=jnp.float32)
        up = jnp.dot(routed_rows, w_up[e], preferred_element_type=jnp.float32)
        hidden.append((jax.nn.silu(gate) * up * mine[:, e : e + 1]).astype(jnp.bfloat16))
    hidden = jnp.concatenate(hidden, axis=1)
    routed = jnp.dot(hidden, w_down.reshape(-1, width), preferred_element_type=jnp.float32)
    routed = by_owner(routed.astype(jnp.bfloat16), owners, half)
    routed = lax.psum_scatter(routed, ("expert", "tensor"), scatter_dimension=0, tiled=True)
    piece = lax.all_gather(normed, "dp", axis=0, tiled=True)
    gate = jnp.dot(piece, shared_gate, preferred_element_type=jnp.float32)
    up = jnp.dot(piece, shared_up, preferred_element_type=jnp.float32)
    shared = (jax.nn.silu(gate) * up).astype(jnp.bfloat16)
    shared = jnp.dot(shared, shared_down, preferred_element_type=jnp.float32)
    shared = by_owner(shared.astype(jnp.bfloat16), groups, half)
    shared = lax.psum_scatter(shared, ("dp", "tensor"), scatter_dimension=0, tiled=True)
    return (shared.astype(jnp.float32) + routed.astype(jnp.float32)).astype(jnp.bfloat16)


def solution(mesh):
    placed = (
        P(("dp", "expert"), None),
        P(),
        P(("dp", "expert"), None),
        P(("dp", "expert"), None),
        P("expert", None, "tensor"),
        P("expert", None, "tensor"),
        P("expert", "tensor", None),
        P(None, ("dp", "tensor")),
        P(None, ("dp", "tensor")),
        P(("dp", "tensor"), None),
    )
    return jax.shard_map(
        on_device,
        mesh=mesh,
        in_specs=placed,
        out_specs=P(("dp", "expert"), "tensor"),
        check_vma=False,
    )
```

profile of v0, /device:TPU:0, one launch (start us, length us, event | category | flops | bytes accessed | tf_op | source)
XLA Modules:
  0.0 212.0 jit_solution(12565851142378850598)
XLA Ops:
  6.6 1.5 fusion.48
  8.0 2.2 %fusion.50 = bf16[128,2560]{1,0:T(8,128)(2,1)} fusion(bf16[128,2560]{1,0:T(8,128)(2,1)} %param.10, f32[2560]{0:T(1024)} %param.11, f32[128]{0:T(128)S(1)} %add_rsqrt_fusion), kind=kLoop, calls=%fused_computation.54 | loop fusion | flops 1310720 | bytes 1321472 | tf_op jit(solution)/shard_map/convert_element_type | solution.py:13
  10.6 2.1 pad_maximum_fusion
  12.7 39.9 %all-gather.3.cloned.1.call-done = bf16[512,2560]{1,0:T(8,128)(2,1)} async-done(((bf16[128,2560]{1,0:T(8,128)(2,1)}), bf16[512,2560]{1,0:T(8,128)(2,1)}) %all-gather.3.cloned.1.call-update) | async-done | bytes 2621456 | tf_op jit(solution)/shard_map/all_gather | solution.py:60
  52.6 2.6 %fusion.171 = f32[512,256]{1,0:T(8,128)S(1)} fusion(bf16[512,2560]{1,0:T(8,128)(2,1)} %all-gather.3.cloned.1.call-done, bf16[2560,256]{1,0:T(8,128)(2,1)S(1)} %copy-done.5), kind=kOutput, calls=%fused_computation.127 | convolution fusion | flops 671088640 | bytes 4456448 | tf_op jit(solution)/shard_map/dot_general | solution.py:61
  55.2 6.4 %convolution_convert_fusion.1 = bf16[512,2560]{1,0:T(8,128)(2,1)} fusion(bf16[256,2560]{1,0:T(8,128)(2,1)S(1)} %copy-done, bf16[512,2560]{1,0:T(8,128)(2,1)} %all-gather.3.cloned.1.call-done, bf16[2560,256]{1,0:T(8,128)(2,1)} %param.18, f32[512,256]{1,0:T(8,128)S(1)} %fusion.171), kind=kOutput, calls=%fused_computation.1 | convolution fusion | flops 1344274432 | bytes 8388608 | tf_op jit(solution)/shard_map/dot_general | solution.py:64
  61.7 5.5 %reshape.26 = bf16[4,128,2,1280]{3,2,1,0:T(2,128)(2,1)S(1)} reshape(bf16[512,2560]{1,0:T(8,128)(2,1)} %convolution_convert_fusion.1) | data formatting | bytes 5242880 | tf_op jit(solution)/shard_map/reshape | solution.py:19
  67.2 1.9 copy.19
  69.3 41.9 %all-gather.5.cloned.1.call-done = bf16[512,2688]{1,0:T(8,128)(2,1)} async-done(((bf16[128,2688]{1,0:T(8,128)(2,1)}), bf16[512,2688]{1,0:T(8,128)(2,1)}) %all-gather.5.cloned.1.call-update) | async-done | bytes 2752528 | tf_op jit(solution)/shard_map/all_gather | solution.py:47
  112.3 1.1 slice_reduce_fusion
  113.5 2.9 %fusion.30 = f32[512,384]{0,1:T(8,128)S(1)} fusion(bf16[8,2560,384]{2,1,0:T(8,128)(2,1)} %param.14, bf16[512,2688]{1,0:T(8,128)(2,1)S(1)} %copy-done.2), kind=kOutput, calls=%fused_computation.32 | convolution fusion | flops 1006632960 | bytes 5373952 | tf_op jit(solution)/shard_map/dot_general | solution.py:53
  116.5 2.9 %fusion.26 = f32[512,384]{0,1:T(8,128)S(1)} fusion(bf16[8,2560,384]{2,1,0:T(8,128)(2,1)} %param.14, bf16[512,2688]{1,0:T(8,128)(2,1)S(1)} %copy-done.2), kind=kOutput, calls=%fused_computation.28 | convolution fusion | flops 1006632960 | bytes 5373952 | tf_op jit(solution)/shard_map/dot_general | solution.py:53
  119.4 3.1 %fusion.22 = f32[512,384]{0,1:T(8,128)S(1)} fusion(bf16[8,2560,384]{2,1,0:T(8,128)(2,1)} %param.14, bf16[512,2688]{1,0:T(8,128)(2,1)S(1)} %copy-done.2), kind=kOutput, calls=%fused_computation.24 | convolution fusion | flops 1006632960 | bytes 5373952 | tf_op jit(solution)/shard_map/dot_general | solution.py:53
  122.6 1.2 fusion.18
  123.8 1.2 fusion.14
  125.1 1.2 fusion.10
  126.3 1.2 fusion.6
  127.6 1.4 slice-done.6
  129.9 2.0 fusion.144
  131.9 2.0 fusion.138
  134.0 2.3 %fusion.132 = bf16[512,3072]{0,1:T(8,128)(2,1)} fusion(bf16[512,3072]{0,1:T(8,128)(2,1)} %fusion.138, bf16[8,2560,384]{2,1,0:T(8,128)(2,1)S(1)} %bitcast.131, f32[512,384]{0,1:T(8,128)S(1)} %fusion.22, f32[512]{0:T(512)S(1)} %get-tuple-element.10, bf16[512,2688]{1,0:T(8,128)(2,1)S(1)} %copy-done.2), kind=kOutput, calls=%fused_computation.82 | convolution fusion | flops 1008009216 | bytes 5769216 | tf_op jit(solution)/shard_map/dot_general | solution.py:54
  136.3 2.1 fusion.126
  138.3 2.0 fusion.120
  140.4 1.2 fusion.2
  141.6 2.1 fusion.114
  143.7 2.0 fusion.108
  145.7 2.1 fusion.102
  147.8 13.0 %convolution_convert_fusion = bf16[512,2560]{1,0:T(8,128)(2,1)S(1)} fusion(bf16[512,3072]{0,1:T(8,128)(2,1)} %fusion.102, bf16[3072,2560]{1,0:T(8,128)(2,1)} %bitcast.132), kind=kOutput, calls=%fused_computation | convolution fusion | flops 8054374400 | bytes 21495808 | tf_op jit(solution)/shard_map/dot_general | solution.py:57
  160.8 2.2 %reshape.29 = bf16[4,128,2,1280]{3,2,1,0:T(2,128)(2,1)} reshape(bf16[512,2560]{1,0:T(8,128)(2,1)S(1)} %convolution_convert_fusion) | data formatting | bytes 5242880 | tf_op jit(solution)/shard_map/reshape | solution.py:19
  163.0 3.7 %copy.20 = bf16[4,2,128,1280]{3,2,1,0:T(8,128)(2,1)} copy(bf16[4,2,128,1280]{3,1,2,0:T(2,128)(2,1)} %bitcast.127) | data formatting | bytes 5242880 | tf_op jit(solution)/shard_map/transpose | solution.py:20
  166.8 36.8 %reduce-scatter.5.cloned.1.call-done = bf16[128,1280]{1,0:T(8,128)(2,1)} async-done(((bf16[1024,1280]{1,0:T(8,128)(2,1)}), bf16[128,1280]{1,0:T(8,128)(2,1)}) %reduce-scatter.5.cloned.1.call-update) | async-done | bytes 327696 | tf_op jit(solution)/shard_map/reduce_scatter | solution.py:59
  203.6 1.9 add_convert_fusion
  (43 shorter events, 2.8 us)
Async XLA Ops:
  6.5 48.7 %copy-start = (bf16[256,2560]{1,0:T(8,128)(2,1)S(1)}, bf16[256,2560]{1,0:T(8,128)(2,1)}, u32[]{:S(2)}) copy-start(bf16[256,2560]{1,0:T(8,128)(2,1)} %param.19) | copy-start | bytes 3932164
  6.5 3.8 %copy-start.4 = (s32[128,6]{0,1:T(8,128)S(1)}, s32[128,6]{0,1:T(8,128)}, u32[]{:S(2)}) copy-start(s32[128,6]{0,1:T(8,128)} %param.12) | copy-start | bytes 9220
  6.5 3.8 %copy-start.3 = (s32[128,6]{0,1:T(8,128)S(1)}, s32[128,6]{0,1:T(8,128)}, u32[]{:S(2)}) copy-start(s32[128,6]{0,1:T(8,128)} %param.13) | copy-start | bytes 9220
  6.5 46.1 %copy-start.5 = (bf16[2560,256]{1,0:T(8,128)(2,1)S(1)}, bf16[2560,256]{1,0:T(8,128)(2,1)}, u32[]{:S(2)}) copy-start(bf16[2560,256]{1,0:T(8,128)(2,1)} %param.17) | copy-start | bytes 3932164
  6.5 46.1 %all-gather.3.cloned.1.call-start = ((), (), s32[]{:S(2)}) async-start(), calls=%async_computation.2 | async-start | bytes 3276800 | tf_op jit(solution)/shard_map/all_gather | solution.py:60
  10.3 100.9 %all-gather.5.cloned.1.call-start = ((), (), s32[]{:S(2)}) async-start(), calls=%async_computation.4 | async-start | bytes 3440640 | tf_op jit(solution)/shard_map/all_gather | solution.py:47
  12.7 154.1 %reduce-scatter.3.cloned.1.call-start = ((), (), s32[]{:S(2)}) async-start(), calls=%async_computation.3 | async-start | bytes 2949120 | tf_op jit(solution)/shard_map/reduce_scatter | solution.py:66
  69.1 134.5 %reduce-scatter.5.cloned.1.call-start = ((), (), s32[]{:S(2)}) async-start(), calls=%async_computation.5 | async-start | bytes 2949120 | tf_op jit(solution)/shard_map/reduce_scatter | solution.py:59
  111.2 2.3 %copy-start.2 = (bf16[512,2688]{1,0:T(8,128)(2,1)S(1)}, bf16[512,2688]{1,0:T(8,128)(2,1)}, u32[]{:S(2)}) copy-start(bf16[512,2688]{1,0:T(8,128)(2,1)} %all-gather.5.cloned.1.call-done) | copy-start | bytes 8257540
  113.5 9.0 %slice-start = ((s8[15728640]{0:T(1024)(128)(4,1)}), s8[4194304]{0:T(1024)(128)(4,1)S(1)}, s32[]{:S(2)}) async-start(s8[15728640]{0:T(1024)(128)(4,1)} %bitcast.128), calls=%async_computation.6 | async-start | bytes 8388608
  113.5 9.0 %slice-start.1 = ((s8[15728640]{0:T(1024)(128)(4,1)}), s8[4194304]{0:T(1024)(128)(4,1)S(1)}, s32[]{:S(2)}) async-start(s8[15728640]{0:T(1024)(128)(4,1)} %bitcast.128), calls=%async_computation.7 | async-start | bytes 8388608
  116.4 6.1 %slice-start.2 = ((s8[15728640]{0:T(1024)(128)(4,1)}), s8[4194304]{0:T(1024)(128)(4,1)S(1)}, s32[]{:S(2)}) async-start(s8[15728640]{0:T(1024)(128)(4,1)} %bitcast.128), calls=%async_computation.8 | async-start | bytes 8388608
  119.4 3.1 %slice-start.3 = ((s8[15728640]{0:T(1024)(128)(4,1)}), s8[3145728]{0:T(1024)(128)(4,1)S(1)}, s32[]{:S(2)}) async-start(s8[15728640]{0:T(1024)(128)(4,1)} %bitcast.128), calls=%async_computation.9 | async-start | bytes 6291456
  123.8 3.8 %slice-start.4 = ((s8[15728640]{0:T(1024)(128)(4,1)}), s8[4194304]{0:T(1024)(128)(4,1)S(1)}, s32[]{:S(2)}) async-start(s8[15728640]{0:T(1024)(128)(4,1)} %bitcast.130), calls=%async_computation.10 | async-start | bytes 8388608
  123.8 3.8 %slice-start.5 = ((s8[15728640]{0:T(1024)(128)(4,1)}), s8[4194304]{0:T(1024)(128)(4,1)S(1)}, s32[]{:S(2)}) async-start(s8[15728640]{0:T(1024)(128)(4,1)} %bitcast.130), calls=%async_computation.11 | async-start | bytes 8388608
  125.0 4.0 %slice-start.6 = ((s8[15728640]{0:T(1024)(128)(4,1)}), s8[4194304]{0:T(1024)(128)(4,1)S(1)}, s32[]{:S(2)}) async-start(s8[15728640]{0:T(1024)(128)(4,1)} %bitcast.130), calls=%async_computation.12 | async-start | bytes 8388608
  126.3 3.6 %slice-start.7 = ((s8[15728640]{0:T(1024)(128)(4,1)}), s8[3145728]{0:T(1024)(128)(4,1)S(1)}, s32[]{:S(2)}) async-start(s8[15728640]{0:T(1024)(128)(4,1)} %bitcast.130), calls=%async_computation.13 | async-start | bytes 6291456
  163.0 42.4 %copy-start.1 = (bf16[256,2560]{1,0:T(8,128)(2,1)S(1)}, bf16[256,2560]{1,0:T(8,128)(2,1)}, u32[]{:S(2)}) copy-start(bf16[256,2560]{1,0:T(8,128)(2,1)} %param.19) | copy-start | bytes 3932164
Sparse Core Ops, SparseCore 0:
  10.4 42.2 all-gather.2
  54.2 56.9 all-gather.4
  114.5 42.2 reduce-scatter.2
  166.8 36.6 reduce-scatter.4
where the time goes:
time: 212 us
  waiting for transfers between devices  119 us (56%)
  matrix products  53.8 us (25%)
  local copies, waits for them, and re-layouts  17.9 us (8%)
  between operations  13.4 us (6%)
  other arithmetic  7.95 us (4%)
    all_gather x1, waiting for transfers between devices, on_device(): everyone = lax.all_gather(sent, 'expert', axis=0, tiled=True)  41.9 us
    all_gather x1, waiting for transfers between devices, on_device(): piece = lax.all_gather(normed, 'dp', axis=0, tiled=True)  39.9 us
    reduce_scatter x1, waiting for transfers between devices, on_device(): lax.psum_scatter(routed, ('expert', 'tensor'), scatter_dimension=0, tiled...  36.8 us
    dot_general x8, matrix products, on_device(): up = jnp.dot(routed_rows, w_up[e], preferred_element_type=jnp.float32)  16.7 us
    dot_general x8, matrix products, on_device(): gate = jnp.dot(routed_rows, w_gate[e], preferred_element_type=jnp.float32)  15.1 us
    dot_general x1, matrix products, on_device(): jnp.dot(hidden, w_down.reshape(-1, width), preferred_element_type=jnp.flo...  13 us
    reshape x2, local copies, waits for them, and re-layouts, by_owner(): split = partial.reshape(blocks, rows, parts, width)  7.73 us
    dot_general x1, matrix products, on_device(): shared = jnp.dot(shared, shared_down, preferred_element_type=jnp.float32)  6.44 us
  transfers between devices with their start and end apart: 4, of which 3 were waited for; matrix products, arithmetic and copies ran while one was open for 34% of the time, Pallas kernels for 0%

commit v1 on v0

--- a/solution.py
+++ b/solution.py
@@ -2,6 +2,7 @@
 import jax.numpy as jnp
 from jax import lax
 from jax.sharding import PartitionSpec as P
+from jax.lax import axis_index, axis_size, ppermute
 
 EPSILON = 1e-06
 LANES = 128
@@ -44,7 +45,19 @@
     scale = jnp.sum(jnp.where(match, route_weights[:, :, None], 0), axis=1)
     scale = (scale.astype(jnp.float32) / 64.0).astype(jnp.bfloat16)
     sent = jnp.concatenate([normed, scale], axis=1)
-    everyone = lax.all_gather(sent, "expert", axis=0, tiled=True)
+
+    def pair_columns_in(vec, along_axis):
+        num_devices = axis_size(along_axis)
+        near = vec
+        buffers = [near]
+        z1 = [(dev - 1, dev) for dev in range(1, num_devices)] + [(num_devices - 1, 0)]
+        for _ in range(num_devices - 1):
+            near = ppermute(near, along_axis, z1)
+            buffers += [near]
+        upper = jnp.concatenate([*reversed(buffers)], axis=0)
+        return jnp.roll(upper, (axis_index(along_axis) + 1) * near.shape[0], axis=0)
+
+    everyone = pair_columns_in(sent, "expert")
     routed_rows = everyone[:, :width]
     first = lax.axis_index("expert") * local
     mine = lax.dynamic_slice_in_dim(everyone[:, width:], first, local, 1).astype(jnp.float32)

time: 212 us -> 223 us (1.052)
  local copies, waits for them, and re-layouts: 17.9 us -> 25.7 us
  matrix products: 53.8 us -> 57.8 us
  waiting for transfers between devices: 119 us -> 115 us
  starting transfers between devices: 0.34 us -> 3.2 us
    ppermute x0 -> x3, waiting for transfers between devices: none -> 53.4 us  [pair_columns_in(): near = ppermute(near, along_axis, z1)]
    reduce_scatter x1, waiting for transfers between devices: 0.02 us -> 45.7 us  [on_device(): lax.psum_scatter(shared, ('dp', 'tensor'), scatter_dimension=0, tiled=True)]
    all_gather x1 -> x0, waiting for transfers between devices: 41.9 us -> none  [on_device(): everyone = lax.all_gather(sent, 'expert', axis=0, tiled=True)]
    all_gather x1, waiting for transfers between devices: 39.9 us -> 0.02 us  [on_device(): piece = lax.all_gather(normed, 'dp', axis=0, tiled=True)]
    reduce_scatter x1, waiting for transfers between devices: 36.8 us -> 15.8 us  [on_device(): lax.psum_scatter(routed, ('expert', 'tensor'), scatter_dimension=0, tiled...]
    reshape x2, local copies, waits for them, and re-layouts: 7.73 us -> 13.3 us  [by_owner(): split = partial.reshape(blocks, rows, parts, width)]
    dot_general x8, matrix products: 15.1 us -> 18.9 us  [on_device(): gate = jnp.dot(routed_rows, w_gate[e], preferred_element_type=jnp.float32)]
    ppermute x0 -> x3, starting transfers between devices: none -> 3.11 us  [pair_columns_in(): near = ppermute(near, along_axis, z1)]
  transfers between devices with their start and end apart: 4 -> 6, of which waited for: 3 -> 5; matrix products, arithmetic and copies ran while one was open for 34% -> 37% of each run, Pallas kernels for 0% -> 0%
where the time goes in v1:
time: 223 us
  waiting for transfers between devices  115 us (52%)
  matrix products  57.8 us (26%)
  local copies, waits for them, and re-layouts  25.7 us (12%)
  between operations  15.2 us (7%)
  other arithmetic  5.9 us (3%)
  starting transfers between devices  3.2 us (1%)
    ppermute x3, waiting for transfers between devices, pair_columns_in(): near = ppermute(near, along_axis, z1)  53.4 us
    reduce_scatter x1, waiting for transfers between devices, on_device(): lax.psum_scatter(shared, ('dp', 'tensor'), scatter_dimension=0, tiled=True)  45.7 us
    dot_general x8, matrix products, on_device(): gate = jnp.dot(routed_rows, w_gate[e], preferred_element_type=jnp.float32)  18.9 us
    dot_general x8, matrix products, on_device(): up = jnp.dot(routed_rows, w_up[e], preferred_element_type=jnp.float32)  16.3 us
    reduce_scatter x1, waiting for transfers between devices, on_device(): lax.psum_scatter(routed, ('expert', 'tensor'), scatter_dimension=0, tiled...  15.8 us
    dot_general x1, matrix products, on_device(): jnp.dot(hidden, w_down.reshape(-1, width), preferred_element_type=jnp.flo...  13.3 us
    reshape x2, local copies, waits for them, and re-layouts, by_owner(): split = partial.reshape(blocks, rows, parts, width)  13.3 us
    transpose x2, local copies, waits for them, and re-layouts, by_owner(): return split.transpose(0, 2, 1, 3).reshape(blocks * parts * rows, width)  7.3 us
  transfers between devices with their start and end apart: 6, of which 5 were waited for; matrix products, arithmetic and copies ran while one was open for 37% of the time, Pallas kernels for 0%

profile of v1, /device:TPU:0, one launch (start us, length us, event | category | flops | bytes accessed | tf_op | source)
XLA Modules:
  0.0 222.7 jit_solution(3615654647368105661)
XLA Ops:
  8.5 1.3 fusion.48
  9.8 1.3 fusion.50
  11.2 3.1 %collective-permute-start = (bf16[128,2688]{1,0:T(8,128)(2,1)S(1)}, bf16[128,2688]{1,0:T(8,128)(2,1)S(1)}, u32[]{:S(2)}, u32[]{:S(2)}) collective-permute-start(bf16[128,2688]{1,0:T(8,128)(2,1)S(1)} %pad_maximum_fusion), channel_id=1, source_target_pairs={{0,2},{2,4},{4,6},{6,0},{1,3},{3,5},{5,7},{7,1},{8,10},{10,12},{12... | collective-permute-start | bytes 2064392 | tf_op jit(solution)/shard_map/ppermute | solution.py:55
  14.3 17.5 %collective-permute-done = bf16[128,2688]{1,0:T(8,128)(2,1)S(1)} collective-permute-done((bf16[128,2688]{1,0:T(8,128)(2,1)S(1)}, bf16[128,2688]{1,0:T(8,128)(2,1)S(1)}, u32[]{:S(2)}, u32[]{:S(2)}) %collective-permute-start) | collective-permute-done | bytes 688160 | tf_op jit(solution)/shard_map/ppermute | solution.py:55
  31.7 18.4 %collective-permute-done.1 = bf16[128,2688]{1,0:T(8,128)(2,1)S(1)} collective-permute-done((bf16[128,2688]{1,0:T(8,128)(2,1)S(1)}, bf16[128,2688]{1,0:T(8,128)(2,1)S(1)}, u32[]{:S(2)}, u32[]{:S(2)}) %collective-permute-start.1) | collective-permute-done | bytes 688160 | tf_op jit(solution)/shard_map/ppermute | solution.py:55
  50.2 17.5 %collective-permute-done.2 = bf16[128,2688]{1,0:T(8,128)(2,1)} collective-permute-done((bf16[128,2688]{1,0:T(8,128)(2,1)S(1)}, bf16[128,2688]{1,0:T(8,128)(2,1)}, u32[]{:S(2)}, u32[]{:S(2)}) %collective-permute-start.2) | collective-permute-done | bytes 688160 | tf_op jit(solution)/shard_map/ppermute | solution.py:55
  69.2 1.3 constant_dynamic-update-slice_fusion.3
  70.8 4.1 %fusion.30 = f32[512,384]{0,1:T(8,128)} fusion(bf16[8,2560,384]{2,1,0:T(8,128)(2,1)} %param.14, bf16[1024,2688]{1,0:T(8,128)(2,1)S(1)} %constant_dynamic-update-slice_fusion, s32[]{:T(128)S(6)} %select_n.22), kind=kOutput, calls=%fused_computation.32 | convolution fusion | flops 1006632960 | bytes 5373956 | tf_op jit(solution)/shard_map/dot_general | solution.py:66
  76.0 2.1 fusion.26
  78.1 2.1 fusion.22
  80.3 2.1 fusion.18
  82.4 2.1 fusion.14
  84.5 2.1 fusion.10
  86.6 2.1 fusion.6
  90.0 2.4 %fusion.57 = bf16[512,3072]{0,1:T(8,128)(2,1)S(1)} fusion(f32[512,384]{0,1:T(8,128)} %fusion.30, f32[512]{0:T(512)S(1)} %get-tuple-element.12, bf16[8,2560,384]{2,1,0:T(8,128)(2,1)S(1)} %bitcast.81, bf16[1024,2688]{1,0:T(8,128)(2,1)S(1)} %constant_dynamic-update-slice_fusion, s32[]{:T(128)S(6)} %select_n.22), kind=kOutput, calls=%fused_computation.72 | convolution fusion | flops 1008009216 | bytes 5769220 | tf_op jit(solution)/shard_map/dot_general | solution.py:67
  92.5 2.6 %fusion.58 = bf16[512,3072]{0,1:T(8,128)(2,1)S(1)} fusion(bf16[512,3072]{0,1:T(8,128)(2,1)S(1)} %fusion.57, f32[512,384]{0,1:T(8,128)} %fusion.26, f32[512]{0:T(512)S(1)} %get-tuple-element.11, bf16[8,2560,384]{2,1,0:T(8,128)(2,1)S(1)} %bitcast.81, bf16[1024,2688]{1,0:T(8,128)(2,1)S(1)} %constant_dynamic-update-slice_fusion, s32[]{:T(128)S(6)} %select_n.22), kind=kOutput, calls=%fused_computation.73 | convolution fusion | flops 1008009216 | bytes 5769220 | tf_op jit(solution)/shard_map/dot_general | solution.py:67
  95.1 2.4 %fusion.59 = bf16[512,3072]{0,1:T(8,128)(2,1)S(1)} fusion(bf16[512,3072]{0,1:T(8,128)(2,1)S(1)} %fusion.58, f32[512,384]{0,1:T(8,128)} %fusion.22, f32[512]{0:T(512)S(1)} %get-tuple-element.10, bf16[8,2560,384]{2,1,0:T(8,128)(2,1)S(1)} %bitcast.81, bf16[1024,2688]{1,0:T(8,128)(2,1)S(1)} %constant_dynamic-update-slice_fusion, s32[]{:T(128)S(6)} %select_n.22), kind=kOutput, calls=%fused_computation.74 | convolution fusion | flops 1008009216 | bytes 5769220 | tf_op jit(solution)/shard_map/dot_general | solution.py:67
  97.5 2.4 %fusion.60 = bf16[512,3072]{0,1:T(8,128)(2,1)S(1)} fusion(bf16[512,3072]{0,1:T(8,128)(2,1)S(1)} %fusion.59, f32[512,384]{0,1:T(8,128)} %fusion.18, f32[512]{0:T(512)S(1)} %get-tuple-element.9, bf16[8,2560,384]{2,1,0:T(8,128)(2,1)S(1)} %bitcast.81, bf16[1024,2688]{1,0:T(8,128)(2,1)S(1)} %constant_dynamic-update-slice_fusion, s32[]{:T(128)S(6)} %select_n.22), kind=kOutput, calls=%fused_computation.75 | convolution fusion | flops 1008009216 | bytes 5769220 | tf_op jit(solution)/shard_map/dot_general | solution.py:67
  100.0 2.1 fusion.2
  102.1 2.5 %fusion.61 = bf16[512,3072]{0,1:T(8,128)(2,1)S(1)} fusion(bf16[512,3072]{0,1:T(8,128)(2,1)S(1)} %fusion.60, f32[512,384]{0,1:T(8,128)} %fusion.14, f32[512]{0:T(512)S(1)} %get-tuple-element.8, bf16[8,2560,384]{2,1,0:T(8,128)(2,1)S(1)} %bitcast.81, bf16[1024,2688]{1,0:T(8,128)(2,1)S(1)} %constant_dynamic-update-slice_fusion, s32[]{:T(128)S(6)} %select_n.22), kind=kOutput, calls=%fused_computation.76 | convolution fusion | flops 1008009216 | bytes 5769220 | tf_op jit(solution)/shard_map/dot_general | solution.py:67
  104.7 1.3 fusion.62
  106.0 1.3 fusion.63
  108.6 13.3 %convolution_convert_fusion = bf16[512,2560]{1,0:T(8,128)(2,1)} fusion(bf16[512,3072]{0,1:T(8,128)(2,1)S(1)} %fusion.64, bf16[3072,2560]{1,0:T(8,128)(2,1)} %bitcast.82), kind=kOutput, calls=%fused_computation | convolution fusion | flops 8054374400 | bytes 21495808 | tf_op jit(solution)/shard_map/dot_general | solution.py:70
  121.9 6.6 %reshape.29 = bf16[4,128,2,1280]{3,2,1,0:T(2,128)(2,1)} reshape(bf16[512,2560]{1,0:T(8,128)(2,1)} %convolution_convert_fusion) | data formatting | bytes 5242880 | tf_op jit(solution)/shard_map/reshape | solution.py:20
  128.6 3.7 %copy.20 = bf16[4,2,128,1280]{3,2,1,0:T(8,128)(2,1)} copy(bf16[4,2,128,1280]{3,1,2,0:T(2,128)(2,1)} %bitcast.78) | data formatting | bytes 5242880 | tf_op jit(solution)/shard_map/transpose | solution.py:21
  132.4 2.6 %fusion.83 = f32[512,256]{1,0:T(8,128)S(1)} fusion(bf16[512,2560]{1,0:T(8,128)(2,1)} %all-gather.2.cloned.1.call-done, bf16[2560,256]{1,0:T(8,128)(2,1)S(1)} %copy-done.4), kind=kOutput, calls=%fused_computation.104 | convolution fusion | flops 671088640 | bytes 4456448 | tf_op jit(solution)/shard_map/dot_general | solution.py:74
  135.0 6.7 %convolution_convert_fusion.1 = bf16[512,2560]{1,0:T(8,128)(2,1)} fusion(bf16[256,2560]{1,0:T(8,128)(2,1)S(1)} %copy-done, bf16[512,2560]{1,0:T(8,128)(2,1)} %all-gather.2.cloned.1.call-done, bf16[2560,256]{1,0:T(8,128)(2,1)} %param.18, f32[512,256]{1,0:T(8,128)S(1)} %fusion.83), kind=kOutput, calls=%fused_computation.1 | convolution fusion | flops 1344274432 | bytes 8388608 | tf_op jit(solution)/shard_map/dot_general | solution.py:77
  141.7 6.7 %reshape.26 = bf16[4,128,2,1280]{3,2,1,0:T(2,128)(2,1)} reshape(bf16[512,2560]{1,0:T(8,128)(2,1)} %convolution_convert_fusion.1) | data formatting | bytes 5242880 | tf_op jit(solution)/shard_map/reshape | solution.py:20
  148.3 3.6 %copy.19 = bf16[4,2,128,1280]{3,2,1,0:T(8,128)(2,1)} copy(bf16[4,2,128,1280]{3,1,2,0:T(2,128)(2,1)} %bitcast.79) | data formatting | bytes 5242880 | tf_op jit(solution)/shard_map/transpose | solution.py:21
  152.0 15.8 %reduce-scatter.5.cloned.1.call-done = bf16[128,1280]{1,0:T(8,128)(2,1)} async-done(((bf16[1024,1280]{1,0:T(8,128)(2,1)}), bf16[128,1280]{1,0:T(8,128)(2,1)}) %reduce-scatter.5.cloned.1.call-update) | async-done | bytes 327696 | tf_op jit(solution)/shard_map/reduce_scatter | solution.py:72
  167.7 45.7 %reduce-scatter.3.cloned.1.call-done = bf16[128,1280]{1,0:T(8,128)(2,1)} async-done(((bf16[1024,1280]{1,0:T(8,128)(2,1)}), bf16[128,1280]{1,0:T(8,128)(2,1)}) %reduce-scatter.3.cloned.1.call-update) | async-done | bytes 327696 | tf_op jit(solution)/shard_map/reduce_scatter | solution.py:79
  213.4 1.9 add_convert_fusion
  (48 shorter events, 6.7 us)
Async XLA Ops:
  7.4 127.6 %copy-start = (bf16[256,2560]{1,0:T(8,128)(2,1)S(1)}, bf16[256,2560]{1,0:T(8,128)(2,1)}, u32[]{:S(2)}) copy-start(bf16[256,2560]{1,0:T(8,128)(2,1)} %param.19) | copy-start | bytes 3932164
  7.4 125.0 %all-gather.2.cloned.1.call-start = ((), (), s32[]{:S(2)}) async-start(), calls=%async_computation.2 | async-start | bytes 3276800 | tf_op jit(solution)/shard_map/all_gather | solution.py:73
  11.1 39.0 %copy-start.1 = (bf16[128,2560]{1,0:T(8,128)(2,1)}, bf16[128,2560]{1,0:T(8,128)(2,1)S(1)}, u32[]{:S(2)}) copy-start(bf16[128,2560]{1,0:T(8,128)(2,1)S(1)} %fusion.50) | copy-start | bytes 1966084
  11.2 20.6 %collective-permute-start = (bf16[128,2688]{1,0:T(8,128)(2,1)S(1)}, bf16[128,2688]{1,0:T(8,128)(2,1)S(1)}, u32[]{:S(2)}, u32[]{:S(2)}) collective-permute-start(bf16[128,2688]{1,0:T(8,128)(2,1)S(1)} %pad_maximum_fusion), channel_id=1, source_target_pairs={{0,2},{2,4},{4,6},{6,0},{1,3},{3,5},{5,7},{7,1},{8,10},{10,12},{12... | collective-permute-start | bytes 2064392 | tf_op jit(solution)/shard_map/ppermute | solution.py:55
  31.7 18.4 %collective-permute-start.1 = (bf16[128,2688]{1,0:T(8,128)(2,1)S(1)}, bf16[128,2688]{1,0:T(8,128)(2,1)S(1)}, u32[]{:S(2)}, u32[]{:S(2)}) collective-permute-start(bf16[128,2688]{1,0:T(8,128)(2,1)S(1)} %collective-permute-done), channel_id=1, source_target_pairs={{0,2},{2,4},{4,6},{6,0},{1,3},{3,5},{5,7},{7,1},{8,10},{10,12},{12... | collective-permute-start | bytes 2064392 | tf_op jit(solution)/shard_map/ppermute | solution.py:55
  50.1 17.6 %collective-permute-start.2 = (bf16[128,2688]{1,0:T(8,128)(2,1)S(1)}, bf16[128,2688]{1,0:T(8,128)(2,1)}, u32[]{:S(2)}, u32[]{:S(2)}) collective-permute-start(bf16[128,2688]{1,0:T(8,128)(2,1)S(1)} %collective-permute-done.1), channel_id=1, source_target_pairs={{0,2},{2,4},{4,6},{6,0},{1,3},{3,5},{5,7},{7,1},{8,10},{10,12},{12... | collective-permute-start | bytes 2064392 | tf_op jit(solution)/shard_map/ppermute | solution.py:55
  50.2 18.9 %copy-start.2 = (bf16[128,2560]{1,0:T(8,128)(2,1)S(1)}, bf16[128,2560]{1,0:T(8,128)(2,1)}, u32[]{:S(2)}) copy-start(bf16[128,2560]{1,0:T(8,128)(2,1)} %copy-done.1) | copy-start | bytes 1966084
  50.2 117.6 %reduce-scatter.5.cloned.1.call-start = ((), (), s32[]{:S(2)}) async-start(), calls=%async_computation.4 | async-start | bytes 2949120 | tf_op jit(solution)/shard_map/reduce_scatter | solution.py:72
  69.2 6.8 %copy-start.3 = (bf16[8,2560,384]{2,1,0:T(8,128)(2,1)S(1)}, bf16[8,2560,384]{2,1,0:T(8,128)(2,1)}, u32[]{:S(2)}) copy-start(bf16[8,2560,384]{2,1,0:T(8,128)(2,1)} %param.14) | copy-start | bytes 47185924
  82.4 7.6 %slice-start = ((s8[15728640]{0:T(1024)(128)(4,1)}), s8[4194304]{0:T(1024)(128)(4,1)S(1)}, s32[]{:S(2)}) async-start(s8[15728640]{0:T(1024)(128)(4,1)} %bitcast.80), calls=%async_computation.5 | async-start | bytes 8388608
  82.4 7.6 %slice-start.1 = ((s8[15728640]{0:T(1024)(128)(4,1)}), s8[4194304]{0:T(1024)(128)(4,1)S(1)}, s32[]{:S(2)}) async-start(s8[15728640]{0:T(1024)(128)(4,1)} %bitcast.80), calls=%async_computation.6 | async-start | bytes 8388608
  84.5 5.5 %slice-start.2 = ((s8[15728640]{0:T(1024)(128)(4,1)}), s8[4194304]{0:T(1024)(128)(4,1)S(1)}, s32[]{:S(2)}) async-start(s8[15728640]{0:T(1024)(128)(4,1)} %bitcast.80), calls=%async_computation.7 | async-start | bytes 8388608
  86.6 3.4 %slice-start.3 = ((s8[15728640]{0:T(1024)(128)(4,1)}), s8[3145728]{0:T(1024)(128)(4,1)S(1)}, s32[]{:S(2)}) async-start(s8[15728640]{0:T(1024)(128)(4,1)} %bitcast.80), calls=%async_computation.8 | async-start | bytes 6291456
  102.1 2.5 %copy-start.6 = (f32[512,384]{0,1:T(8,128)S(1)}, f32[512,384]{0,1:T(8,128)}, u32[]{:S(2)}) copy-start(f32[512,384]{0,1:T(8,128)} %fusion.10) | copy-start | bytes 2359300
  104.6 1.3 copy-start.5
  106.0 1.3 copy-start.7
  128.6 3.8 %copy-start.4 = (bf16[2560,256]{1,0:T(8,128)(2,1)S(1)}, bf16[2560,256]{1,0:T(8,128)(2,1)}, u32[]{:S(2)}) copy-start(bf16[2560,256]{1,0:T(8,128)(2,1)} %param.17) | copy-start | bytes 3932164
  132.3 81.1 %reduce-scatter.3.cloned.1.call-start = ((), (), s32[]{:S(2)}) async-start(), calls=%async_computation.3 | async-start | bytes 2949120 | tf_op jit(solution)/shard_map/reduce_scatter | solution.py:79
Sparse Core Ops, SparseCore 0:
  50.3 40.7 all-gather.1
Sparse Core Ops, SparseCore 1:
  132.4 35.3 reduce-scatter.4
  170.9 42.4 reduce-scatter.2
